TPU v7x, 32 devices: a whole 2x2x4 slice. The times are simulated.
32 devices in a mesh: ep: 8 (over z, y), dp: 4 (over x, core).
Axes of the slice: x: 2, y: 2, z: 4, core: 2. Of those that a mesh axis runs over, the one named last changes fastest.
Arguments:
- tokens: bfloat16 [4096, 7168], P(('dp', 'ep')), parts along dimension 0, may hold values from -18 to 18
- expert_ids: int32 [4096, 2], P(('dp', 'ep')), parts along dimension 0, may hold values from 0 to 3, all different within a row; in each aligned block of 128 rows (0 to 127, 128 to 255, ...) at most 128 rows name the same one
- affinity: float32 [4096, 2], P(('dp', 'ep')), parts along dimension 0, may hold values from 0.05 to 1
- w_gate: bfloat16 [8, 7168, 512], P('ep'), may hold values from -0.0625 to 0.0625
- w_up: bfloat16 [8, 7168, 512], P('ep'), may hold values from -0.0625 to 0.0625
- w_down: bfloat16 [8, 512, 7168], P('ep'), may hold values from -0.1875 to 0.1875
Outputs:
- mixed: bfloat16 [4096, 7168], P(('dp', 'ep')), parts along dimension 0
There are 4 independent parts, one for each index of `dp`. A program takes and returns all parts, laid end to end along the dimension named above; an argument that names none is the same for every part. Nothing has to cross between parts.
Inputs may be any that keep to these rules, and one draw needn't show every extreme that they name: `expert_ids`: each row names 2 different experts; among the rows of one index of ep no expert is named by more than 128 rows.
All inputs are finite; a program needn't handle non-finite values.
Results may differ from a plain program's by a relative error of at most 0.019.
Values may be sent and summed in bfloat16 or wider, within the bound.
A program may use at most 256 MiB of HBM per device.

v0:
```python
import jax
import jax.numpy as jnp
from jax import lax
from jax.sharding import PartitionSpec as P

TOP = 2
TOK_DEV = 128


def quantize(tokens):
    count_rows = tokens.shape[0]
    blocks = tokens.astype(jnp.float32).reshape(count_rows, -1, 16)
    largest = jnp.max(jnp.abs(blocks), axis=2)
    scales = (jnp.maximum(largest, 0.25) / 9.0).astype(jnp.bfloat16)
    divided = blocks / scales.astype(jnp.float32)[:, :, None]
    payload = jnp.clip(divided, -6.0, 6.0).astype(jnp.bfloat16).reshape(count_rows, -1)
    return (payload, scales)


def restore(payload, scales):
    count_rows = payload.shape[0]
    values = (
        payload.astype(jnp.float32).reshape(count_rows, -1, 16)
        * scales.astype(jnp.float32)[:, :, None]
    )
    return values.astype(jnp.bfloat16).reshape(count_rows, -1)


def half_expert(restored, gate_half, up_half, down_half):
    gate = jnp.dot(restored, gate_half, preferred_element_type=jnp.float32)
    upward = jnp.dot(restored, up_half, preferred_element_type=jnp.float32)
    hidden = (jax.nn.silu(gate) * upward).astype(jnp.bfloat16)
    return jnp.dot(hidden, down_half, preferred_element_type=jnp.float32).astype(jnp.bfloat16)


def expert_rows(payload, scales, gate_half, up_half, down_half):
    return half_expert(restore(payload, scales), gate_half, up_half, down_half)


def on_device(tokens, expert_ids, affinity, w_gate, w_up, w_down):
    ep_count = lax.axis_size("ep")
    experts = ep_count // 2
    capacity = 2 * TOK_DEV * TOP // experts
    tok_rows = tokens.shape[0]
    row_width = tokens.shape[1]
    scale_width = row_width // 16
    gate_half = w_gate[0]
    up_half = w_up[0]
    down_half = w_down[0]
    payload, scales = quantize(tokens)
    flat_ids = expert_ids.reshape(-1)
    assigned = flat_ids.shape[0]
    one_hot = (flat_ids[:, None] == jnp.arange(experts, dtype=jnp.int32)[None, :]).astype(jnp.int32)
    running = jnp.cumsum(one_hot, axis=0) - 1
    within = jnp.sum(running * one_hot, axis=1)
    slot_index = flat_ids * capacity + within
    slot_total = experts * capacity
    source_row = (
        jnp.zeros((slot_total,), jnp.int32)
        .at[slot_index]
        .set(jnp.arange(assigned, dtype=jnp.int32) // TOP)
    )
    filled = jnp.zeros((slot_total,), jnp.int32).at[slot_index].set(1) > 0
    send_payload = jnp.where(filled[:, None], payload[source_row], jnp.zeros((), jnp.bfloat16))
    send_scales = jnp.where(filled[:, None], scales[source_row], jnp.zeros((), jnp.bfloat16))
    doubled_payload = jnp.repeat(send_payload.reshape(experts, capacity, row_width), 2, axis=0)
    doubled_scales = jnp.repeat(send_scales.reshape(experts, capacity, scale_width), 2, axis=0)
    got_payload = lax.all_to_all(doubled_payload, "ep", split_axis=0, concat_axis=0, tiled=True)
    got_scales = lax.all_to_all(doubled_scales, "ep", split_axis=0, concat_axis=0, tiled=True)
    sources = got_payload.shape[0]
    slot_count = got_payload.shape[1]
    computed = expert_rows(
        got_payload.reshape(sources * slot_count, row_width),
        got_scales.reshape(sources * slot_count, scale_width),
        gate_half,
        up_half,
        down_half,
    )
    returned = lax.all_to_all(
        computed.reshape(sources, slot_count, row_width),
        "ep",
        split_axis=0,
        concat_axis=0,
        tiled=True,
    )
    halves = returned.reshape(experts, 2, capacity, row_width).astype(jnp.float32)
    expert_out = (halves[:, 0] + halves[:, 1]).astype(jnp.bfloat16).reshape(slot_total, row_width)
    per_slot = expert_out[slot_index].astype(jnp.float32).reshape(tok_rows, TOP, row_width)
    weights = affinity / jnp.sum(affinity, axis=1, keepdims=True)
    return jnp.sum(weights[:, :, None] * per_slot, axis=1).astype(jnp.bfloat16)


def solution(mesh):
    in_specs = (
        P(("dp", "ep"), None),
        P(("dp", "ep"), None),
        P(("dp", "ep"), None),
        P("ep", None, None),
        P("ep", None, None),
        P("ep", None, None),
    )
    out_specs = P(("dp", "ep"), None)
    return jax.shard_map(
        on_device, mesh=mesh, in_specs=in_specs, out_specs=out_specs, check_vma=False
    )
```

profile of v0, /device:TPU:0, one launch (start us, length us, event | category | flops | bytes accessed | tf_op | source)
XLA Modules:
  0.0 859.4 jit_solution(7512660911354682419)
XLA Ops:
  0.0 0.8 copy.58
  0.8 0.1 eq.29
  0.9 0.1 eq.25
  1.1 0.7 broadcast_multiply_fusion
  1.8 1.2 reduce-window.6
  3.0 0.1 slice.22
  3.1 0.1 copy.60
  3.2 0.1 copy.61
  3.3 0.1 add_bitcast_fusion
  3.4 0.1 copy.57
  3.5 0.1 mul.57
  3.7 1.4 scatter_custom_fusion.1
  5.1 3.7 convert_abs_fusion
  8.8 5.3 copy.62
  14.1 2.6 reduce_max.9
  16.8 1.4 scatter_custom_fusion
  18.2 0.1 copy.66
  18.3 2.0 gather_fusion.1
  20.3 0.1 broadcast_select_fusion.1
  20.4 0.3 copy.67
  20.7 1.0 broadcast_in_dim.57
  21.7 7.3 all-to-all-start.1
  29.0 2.0 div.39
  31.1 5.2 copy.63
  36.3 3.2 fusion.8
  39.5 7.1 gather_fusion
  46.6 6.6 broadcast_select_fusion
  53.3 10.0 %copy.64 = bf16[4,128,7168]{1,2,0:T(8,128)(2,1)} copy(bf16[4,128,7168]{2,1,0:T(8,128)(2,1)} %broadcast_select_fusion) | data formatting | bytes 14680064 | tf_op jit(solution)/shard_map/jit(_where)/select_n | solution.py:64
  63.3 9.9 %broadcast_in_dim.54 = bf16[4,2,128,7168]{2,3,1,0:T(8,128)(2,1)} broadcast(bf16[4,128,7168]{1,2,0:T(8,128)(2,1)} %copy.64), dimensions={0,2,3} | broadcast | bytes 22020096 | tf_op jit(solution)/shard_map/broadcast_in_dim | solution.py:66
  73.2 6.0 all-to-all-start
  79.1 0.2 copy_bitcast_fusion
  79.4 317.4 %all-to-all-done = bf16[8,128,7168]{1,2,0:T(8,128)(2,1)} async-done(((bf16[8,128,7168]{1,2,0:T(8,128)(2,1)}), bf16[8,128,7168]{1,2,0:T(8,128)(2,1)}, u32[]{:S(2)}, u32[]{:S(2)}) %all-to-all-start) | async-done | bytes 14680096 | tf_op jit(solution)/shard_map/all_to_all | solution.py:68
  396.8 19.8 %copy.65 = f32[8,128,7168]{1,0,2:T(8,128)} copy(bf16[8,128,7168]{1,2,0:T(8,128)(2,1)} %all-to-all-done) | data formatting | bytes 44040192 | tf_op jit(solution)/shard_map/convert_element_type | solution.py:23
  416.6 31.1 %reshape.137 = f32[1024,448,16]{0,2,1:T(8,128)} reshape(f32[8,128,7168]{1,0,2:T(8,128)} %copy.65) | data formatting | bytes 58720256 | tf_op jit(solution)/shard_map/convert_element_type | solution.py:23
  447.6 12.0 %multiply_convert_fusion = bf16[1024,448,16]{0,2,1:T(8,128)(2,1)S(1)} fusion(f32[1024,448,16]{0,2,1:T(8,128)} %reshape.137, f32[1024,448]{0,1:T(8,128)S(1)} %copy_bitcast_fusion), kind=kLoop, calls=%fused_computation.5 | loop fusion | flops 14680064 | bytes 45875200 | tf_op jit(solution)/shard_map/convert_element_type | solution.py:26
  459.6 0.0 slice-start
  459.6 10.4 %fusion.3 = f32[1024,512]{1,0:T(8,128)S(1)} fusion(bf16[1024,7168]{0,1:T(8,128)(2,1)S(1)} %bitcast.67, bf16[1,7168,512]{2,1,0:T(8,128)(2,1)} %param.10), kind=kOutput, calls=%fused_computation.12 | convolution fusion | flops 7516192768 | bytes 24117248 | tf_op jit(solution)/shard_map/dot_general | solution.py:31
  470.0 0.0 slice-start.1
  470.0 10.4 %multiply_convert_fusion.1 = bf16[1024,512]{1,0:T(8,128)(2,1)S(1)} fusion(f32[1024,512]{1,0:T(8,128)S(1)} %fusion.3, bf16[1024,7168]{0,1:T(8,128)(2,1)S(1)} %bitcast.68, bf16[1,7168,512]{2,1,0:T(8,128)(2,1)} %param.9), kind=kOutput, calls=%fused_computation.22 | convolution fusion | flops 7519338496 | bytes 25165824 | tf_op jit(solution)/shard_map/dot_general | solution.py:30
  480.4 11.1 %convolution_convert_fusion = bf16[1024,7168]{1,0:T(8,128)(2,1)} fusion(bf16[1024,512]{1,0:T(8,128)(2,1)S(1)} %multiply_convert_fusion.1, bf16[1,512,7168]{2,1,0:T(8,128)(2,1)S(1)} %bitcast.76), kind=kOutput, calls=%fused_computation.10 | convolution fusion | flops 7523532800 | bytes 23068672 | tf_op jit(solution)/shard_map/dot_general | solution.py:33
  491.6 5.7 all-to-all-start.2
  497.3 0.1 copy.56
  497.4 316.5 %all-to-all-done.2 = bf16[8,128,7168]{2,1,0:T(8,128)(2,1)} async-done(((bf16[8,128,7168]{2,1,0:T(8,128)(2,1)}), bf16[8,128,7168]{2,1,0:T(8,128)(2,1)}, u32[]{:S(2)}, u32[]{:S(2)}) %all-to-all-start.2) | async-done | bytes 14680096 | tf_op jit(solution)/shard_map/all_to_all | solution.py:79
  814.0 8.4 convert.4
  822.4 3.9 fusion.1
  826.3 12.1 %gather_fusion.2 = bf16[256,7168]{1,0:T(8,128)(2,1)} fusion(bf16[512,7168]{1,0:T(8,128)(2,1)} %bitcast.61, s32[1024]{0:T(1024)S(1)} %pad_clamp_fusion), kind=kCustom, calls=%fused_computation.2 | custom fusion | bytes 7341056 | tf_op jit(solution)/shard_map/gather | solution.py:88
  838.4 8.6 %reshape.140 = f32[128,2,7168]{2,1,0:T(2,128)} reshape(bf16[256,7168]{1,0:T(8,128)(2,1)} %gather_fusion.2) | data formatting | bytes 11010048 | tf_op jit(solution)/shard_map/convert_element_type | solution.py:88
  847.0 12.4 %multiply_reduce_fusion = bf16[128,7168]{1,0:T(8,128)(2,1)} fusion(f32[128,2,7168]{2,1,0:T(2,128)} %reshape.140, f32[128,2]{1,0:T(8,128)S(1)} %copy.56), kind=kLoop, calls=%fused_computation.16 | loop fusion | flops 2752512 | bytes 9176064 | tf_op jit(solution)/shard_map/reduce_sum | solution.py:90
  (20 shorter events, 0.2 us)
Async XLA Ops:
  21.7 41.5 %all-to-all-start.1 = ((bf16[8,128,448]{1,2,0:T(8,128)(2,1)}), bf16[8,128,448]{1,2,0:T(8,128)(2,1)S(1)}, u32[]{:S(2)}, u32[]{:S(2)}) async-start(bf16[8,128,448]{1,2,0:T(8,128)(2,1)} %bitcast.10), calls=%async_computation.1 | async-start | bytes 1835008 | tf_op jit(solution)/shard_map/all_to_all | solution.py:69
  73.2 323.6 %all-to-all-start = ((bf16[8,128,7168]{1,2,0:T(8,128)(2,1)}), bf16[8,128,7168]{1,2,0:T(8,128)(2,1)}, u32[]{:S(2)}, u32[]{:S(2)}) async-start(bf16[8,128,7168]{1,2,0:T(8,128)(2,1)} %bitcast.62), calls=%async_computation | async-start | bytes 29360128 | tf_op jit(solution)/shard_map/all_to_all | solution.py:68
  459.6 20.8 %slice-start = ((s8[7340032]{0:T(1024)(128)(4,1)}), s8[4194304]{0:T(1024)(128)(4,1)S(1)}, s32[]{:S(2)}) async-start(s8[7340032]{0:T(1024)(128)(4,1)} %bitcast.75), calls=%async_computation.3 | async-start | bytes 8388608
  470.0 10.4 %slice-start.1 = ((s8[7340032]{0:T(1024)(128)(4,1)}), s8[3145728]{0:T(1024)(128)(4,1)S(1)}, s32[]{:S(2)}) async-start(s8[7340032]{0:T(1024)(128)(4,1)} %bitcast.75), calls=%async_computation.4 | async-start | bytes 6291456
  491.6 5.7 copy-start
  491.6 322.4 %all-to-all-start.2 = ((bf16[8,128,7168]{2,1,0:T(8,128)(2,1)}), bf16[8,128,7168]{2,1,0:T(8,128)(2,1)}, u32[]{:S(2)}, u32[]{:S(2)}) async-start(bf16[8,128,7168]{2,1,0:T(8,128)(2,1)} %bitcast.64), calls=%async_computation.2 | async-start | bytes 29360128 | tf_op jit(solution)/shard_map/all_to_all | solution.py:79
where the time goes:
time: 862 us; the launch traced here: 859 us
  waiting for transfers between devices  634 us (74%)
  local copies, waits for them, and re-layouts  119 us (14%)
  other arithmetic  55.2 us (6%)
  matrix products  31.9 us (4%)
  starting transfers between devices  19 us (2%)
    all_to_all x1, waiting for transfers between devices, on_device(): lax.all_to_all(doubled_payload, 'ep', split_axis=0, concat_axis=0, tiled=...  317 us
    all_to_all x1, waiting for transfers between devices, on_device(): lax.all_to_all(computed.reshape(sources, slot_count, row_width), 'ep', sp...  317 us
    convert_element_type x2, local copies, waits for them, and re-layouts, restore(): payload.astype(jnp.float32).reshape(count_rows, -1, 16)  50.9 us
  transfers between devices with their start and end apart: 3, of which 2 were waited for; matrix products, arithmetic and copies ran while one was open for 4% of the time, Pallas kernels for 0%

commit v1 on v0

v1 whole, which is shorter than its diff:
```python
import functools

import jax
import jax.numpy as jnp
from jax import lax
from jax.experimental import pallas as pl
from jax.experimental.pallas import tpu as pltpu
from jax.sharding import PartitionSpec as P

RING = 4
LANES = 128
MESH = pl.DeviceIdType.MESH
VMEM_LIMIT = 48 * 1024 * 1024


def requantized(tokens):
    rows, width = tokens.shape
    blocks = tokens.astype(jnp.float32).reshape(rows, -1, 16)
    largest = jnp.max(jnp.abs(blocks), axis=2)
    scales = (jnp.maximum(largest, 0.25) / 9.0).astype(jnp.bfloat16).astype(jnp.float32)
    divided = blocks / scales[:, :, None]
    payload = jnp.clip(divided, -6.0, 6.0).astype(jnp.bfloat16).astype(jnp.float32)
    return (payload * scales[:, :, None]).astype(jnp.bfloat16).reshape(rows, width)


def split_of(width):
    tiles = width // LANES
    return (tiles * 5 + 4) // 9 * LANES


def places():
    me = lax.axis_index("ep")
    z, y = me // 2, lax.rem(me, 2)
    up, down, far = lax.rem(z + 1, RING), lax.rem(z + 3, RING), lax.rem(z + 2, RING)
    return me, z, y, 1 - y, up, down, far


def meet(targets):
    barrier = pltpu.get_barrier_semaphore()
    for target in targets:
        pl.semaphore_signal(barrier, inc=1, device_id={"ep": target}, device_id_type=MESH)
    pl.semaphore_wait(barrier, len(targets))


def spread(n, x_ref, share_ref, all_ref, shares_ref, send, recv, local):
    me, z, y, other, up, down, far = places()
    rows, width = x_ref.shape
    cut = split_of(width)
    first, second = pl.ds(0, cut), pl.ds(cut, width - cut)
    upper, lower = pl.ds(0, rows // 2), pl.ds(rows // 2, rows // 2)
    full = pl.ds(0, rows)
    to_up, to_down, to_peer = 2 * up + y, 2 * down + y, 2 * z + other

    keep = pltpu.make_async_copy(x_ref, all_ref.at[me], local.at[0])
    keep_share = pltpu.make_async_copy(share_ref, shares_ref.at[me], local.at[1])
    keep.start()
    keep_share.start()
    meet([lax.rem(me + step, n) for step in range(1, n)])
    copies = {}

    def start(name, owner, rows_of, columns, target, own=False):
        k = len(copies)
        place = all_ref.at[owner, rows_of, columns]
        copies[name] = pltpu.make_async_remote_copy(
            src_ref=x_ref.at[rows_of, columns] if own else place,
            dst_ref=place,
            send_sem=send.at[k],
            recv_sem=recv.at[k],
            device_id={"ep": target},
            device_id_type=MESH,
        )
        copies[name].start()

    arrived = []

    def wait(name):
        copies[name].wait_recv()
        arrived.append(name)

    start("b_up", me, full, second, to_up, own=True)
    start("b_down", me, full, second, to_down, own=True)
    start("a_peer", me, full, first, to_peer, own=True)
    for step in range(1, n):
        k = len(copies)
        copies[("share", step)] = pltpu.make_async_remote_copy(
            src_ref=share_ref,
            dst_ref=shares_ref.at[me],
            send_sem=send.at[k],
            recv_sem=recv.at[k],
            device_id={"ep": lax.rem(me + step, n)},
            device_id_type=MESH,
        )
        copies[("share", step)].start()
    start("b_peer", me, full, second, to_peer, own=True)
    start("a_up", me, full, first, to_up, own=True)
    start("a_down", me, full, first, to_down, own=True)
    wait("b_up")
    start("b_up2", 2 * down + y, upper, second, to_up)
    start("b_up_peer", 2 * down + y, full, second, to_peer)
    wait("b_down")
    start("b_down2", 2 * up + y, lower, second, to_down)
    start("b_down_peer", 2 * up + y, full, second, to_peer)
    wait("a_peer")
    start("p_up", 2 * z + other, full, first, to_up)
    start("p_down", 2 * z + other, full, first, to_down)
    wait("a_up")
    start("a_up2", 2 * down + y, upper, first, to_up)
    wait("a_down")
    start("a_down2", 2 * up + y, lower, first, to_down)
    wait("b_up2")
    start("b_up2_peer", 2 * far + y, upper, second, to_peer)
    wait("b_down2")
    start("b_down2_peer", 2 * far + y, lower, second, to_peer)
    wait("p_up")
    start("p_up2", 2 * down + other, upper, first, to_up)
    wait("p_down")
    start("p_down2", 2 * up + other, lower, first, to_down)
    for name in list(copies):
        if name not in arrived:
            wait(name)
    for name in copies:
        copies[name].wait_send()
    keep.wait()
    keep_share.wait()


def all_tokens(restored, share):
    n = lax.axis_size("ep")
    rows, width = restored.shape
    count = 18 + n - 1
    return pl.pallas_call(
        functools.partial(spread, n),
        out_shape=(
            jax.ShapeDtypeStruct((n, rows, width), restored.dtype),
            jax.ShapeDtypeStruct((n,) + share.shape, share.dtype),
        ),
        in_specs=[pl.BlockSpec(memory_space=pltpu.VMEM)] * 2,
        out_specs=[pl.BlockSpec(memory_space=pl.ANY)] * 2,
        scratch_shapes=[
            pltpu.SemaphoreType.DMA((count,)),
            pltpu.SemaphoreType.DMA((count,)),
            pltpu.SemaphoreType.DMA((2,)),
        ],
        compiler_params=pltpu.CompilerParams(
            collective_id=0, has_side_effects=True, vmem_limit_bytes=VMEM_LIMIT
        ),
        name="spread",
    )(restored, share)


def add_up(target, sources):
    rows = target.shape[0]
    step = 16

    def body(i, carry):
        at = pl.ds(pl.multiple_of(i * step, step), step)
        total = sources[0][at, :].astype(jnp.float32)
        for source in sources[1:]:
            total = total + source[at, :].astype(jnp.float32)
        target[at, :] = total.astype(target.dtype)
        return carry

    lax.fori_loop(0, rows // step, body, 0)


def gather_sums(
    c_ref, out_ref, own_b, own_a, end_a, got_b, got_b1, got_b2, got_a1, got_a2, got_a3,
    send, recv, local,
):
    me, z, y, other, up, down, far = places()
    rows, width = out_ref.shape
    half = rows // 2
    cut = split_of(width)
    first, second = pl.ds(0, cut), pl.ds(cut, width - cut)
    full, upper, lower = pl.ds(0, rows), pl.ds(0, half), pl.ds(half, half)
    to_up, to_down, to_peer = 2 * up + y, 2 * down + y, 2 * z + other
    faces = (other, y)
    loads = {}
    copies = {}

    def load(name, owner, rows_of, columns, place):
        k = len(loads)
        loads[name] = pltpu.make_async_copy(
            c_ref.at[owner, rows_of, columns], place, local.at[k]
        )
        loads[name].start()

    def start(name, source, place, target):
        k = len(copies)
        copies[name] = pltpu.make_async_remote_copy(
            src_ref=source,
            dst_ref=place,
            send_sem=send.at[k],
            recv_sem=recv.at[k],
            device_id={"ep": target},
            device_id_type=MESH,
        )
        copies[name].start()

    def arrive(*names):
        for name in names:
            copies[name].wait_recv()

    for i in range(2):
        load(("a_up", i), 2 * up + faces[i], upper, first, own_a.at[0, i])
        load(("a_down", i), 2 * down + faces[i], lower, first, own_a.at[1, i])
    for i, place in enumerate((far, up, down, z)):
        load(("b", i), 2 * place + y, full, second, own_b.at[i])
    for i in range(2):
        load(("a", i), 2 * z + faces[i], full, first, end_a.at[i])
    meet([to_up, to_down, to_peer])
    start(("b", 0), c_ref.at[2 * far + other, full, second], got_b.at[0], to_peer)
    for i in range(2):
        owner = 2 * far + faces[i]
        start(("a1_up", i), c_ref.at[owner, upper, first], got_a1.at[0, i], to_up)
        start(("a1_down", i), c_ref.at[owner, lower, first], got_a1.at[1, i], to_down)
    for i, place in ((1, up), (2, down), (3, z)):
        start(("b", i), c_ref.at[2 * place + other, full, second], got_b.at[i], to_peer)
    for i in range(2):
        start(("r_up", i), c_ref.at[2 * up + faces[i], lower, first], got_a2.at[0, i, lower], to_up)
        start(("r_down", i), c_ref.at[2 * down + faces[i], upper, first], got_a2.at[1, i, upper], to_down)
    for name in loads:
        loads[name].wait()

    def pass_a(i):
        arrive(("a1_up", i))
        add_up(own_a.at[0, i], [own_a.at[0, i], got_a1.at[0, i]])
        start(("a2_up", i), own_a.at[0, i], got_a2.at[0, i, upper], to_up)
        arrive(("a1_down", i))
        add_up(own_a.at[1, i], [own_a.at[1, i], got_a1.at[1, i]])
        start(("a2_down", i), own_a.at[1, i], got_a2.at[1, i, lower], to_down)

    pass_a(0)
    arrive(("b", 0))
    add_up(own_b.at[0], [own_b.at[0], got_b.at[0]])
    start("b1_up", own_b.at[0, upper], got_b1.at[0], to_up)
    start("b1_down", own_b.at[0, lower], got_b1.at[1], to_down)
    pass_a(1)
    arrive(("b", 1), ("b", 2))
    add_up(own_b.at[1, lower], [own_b.at[1, lower], got_b.at[1, lower]])
    add_up(own_b.at[2, upper], [own_b.at[2, upper], got_b.at[2, upper]])
    arrive(("r_up", 0), ("r_down", 0), ("a2_up", 0), ("a2_down", 0))
    add_up(end_a.at[0], [end_a.at[0], got_a2.at[0, 0], got_a2.at[1, 0]])
    start("a3", end_a.at[0], got_a3, to_peer)
    arrive("b1_up")
    add_up(own_b.at[1, upper], [own_b.at[1, upper], got_b.at[1, upper], got_b1.at[0]])
    start("b2_up", own_b.at[1], got_b2.at[0], to_up)
    arrive("b1_down")
    add_up(own_b.at[2, lower], [own_b.at[2, lower], got_b.at[2, lower], got_b1.at[1]])
    start("b2_down", own_b.at[2], got_b2.at[1], to_down)
    arrive(("r_up", 1), ("r_down", 1), ("a2_up", 1), ("a2_down", 1))
    arrive(("b", 3), "a3")
    add_up(out_ref.at[:, first], [end_a.at[1], got_a2.at[0, 1], got_a2.at[1, 1], got_a3])
    arrive("b2_up", "b2_down")
    add_up(out_ref.at[:, second], [own_b.at[3], got_b.at[3], got_b2.at[0], got_b2.at[1]])
    for name in copies:
        copies[name].wait_send()


def summed(scaled):
    n, rows, width = scaled.shape
    half = rows // 2
    cut = split_of(width)
    rest = width - cut
    kind = scaled.dtype
    return pl.pallas_call(
        gather_sums,
        out_shape=jax.ShapeDtypeStruct((rows, width), kind),
        in_specs=[pl.BlockSpec(memory_space=pl.ANY)],
        out_specs=pl.BlockSpec(memory_space=pltpu.VMEM),
        scratch_shapes=[
            pltpu.VMEM((4, rows, rest), kind),
            pltpu.VMEM((2, 2, half, cut), kind),
            pltpu.VMEM((2, rows, cut), kind),
            pltpu.VMEM((4, rows, rest), kind),
            pltpu.VMEM((2, half, rest), kind),
            pltpu.VMEM((2, rows, rest), kind),
            pltpu.VMEM((2, 2, half, cut), kind),
            pltpu.VMEM((2, 2, rows, cut), kind),
            pltpu.VMEM((rows, cut), kind),
            pltpu.SemaphoreType.DMA((21,)),
            pltpu.SemaphoreType.DMA((21,)),
            pltpu.SemaphoreType.DMA((10,)),
        ],
        compiler_params=pltpu.CompilerParams(
            collective_id=1, has_side_effects=True, vmem_limit_bytes=VMEM_LIMIT
        ),
        name="gather_sums",
    )(scaled)


def on_device(tokens, expert_ids, affinity, w_gate, w_up, w_down):
    n = lax.axis_size("ep")
    experts = n // 2
    own = lax.axis_index("ep") // 2
    rows, width = tokens.shape
    restored = requantized(tokens)
    weights = affinity / jnp.sum(affinity, axis=1, keepdims=True)
    padded = -(-experts // 8) * 8
    names = jnp.arange(padded, dtype=jnp.int32)[:, None]
    shares = sum(
        jnp.where(expert_ids[:, k][None, :] == names, weights[:, k][None, :], 0.0)
        for k in range(weights.shape[1])
    )
    by_ring = experts == RING and rows % 32 == 0 and width % LANES == 0
    if by_ring:
        every, shares = all_tokens(restored, shares)
    else:
        every = lax.all_gather(restored, "ep", axis=0, tiled=False)
        shares = lax.all_gather(shares, "ep", axis=0, tiled=False)
    every = every.reshape(n * rows, width)
    share = lax.dynamic_slice_in_dim(shares, own, 1, axis=1).reshape(n * rows, 1)
    gate = jnp.dot(every, w_gate[0], preferred_element_type=jnp.float32)
    upward = jnp.dot(every, w_up[0], preferred_element_type=jnp.float32)
    hidden = (jax.nn.silu(gate) * upward).astype(jnp.bfloat16)
    partial = jnp.dot(hidden, w_down[0], preferred_element_type=jnp.float32)
    scaled = (partial * share).astype(jnp.bfloat16)
    if by_ring:
        return summed(scaled.reshape(n, rows, width))
    return lax.psum_scatter(scaled, "ep", scatter_dimension=0, tiled=True)


def solution(mesh):
    in_specs = (
        P(("dp", "ep"), None),
        P(("dp", "ep"), None),
        P(("dp", "ep"), None),
        P("ep", None, None),
        P("ep", None, None),
        P("ep", None, None),
    )
    return jax.shard_map(
        on_device, mesh=mesh, in_specs=in_specs, out_specs=P(("dp", "ep"), None), check_vma=False
    )
```

time: 862 us -> 442 us (0.51)
  waiting for transfers between devices: 634 us -> 0 us
  Pallas kernels: 0 us -> 378 us
  local copies, waits for them, and re-layouts: 119 us -> 14.7 us
  other arithmetic: 55.2 us -> 10.5 us
  starting transfers between devices: 19 us -> 0 us
    all_to_all x3 -> x0, waiting for transfers between devices: 634 us -> none  [the longest x1 317 us: on_device(): lax.all_to_all(doubled_payload, 'ep', split_axis=0, concat_axis=0, tiled=...]
    pallas_call x0 -> x2, Pallas kernels: none -> 378 us  [the longest x1 191 us: all_tokens(): pl.pallas_call(functools.partial(spread, n), out_shape=(jax.ShapeDtypeStr...]
    convert_element_type x4 -> x0, local copies, waits for them, and re-layouts: 59.6 us -> none  [the longest x2 50.9 us: restore(): payload.astype(jnp.float32).reshape(count_rows, -1, 16)]
    convert_element_type x7 -> x2, other arithmetic: 27.7 us -> 2.81 us  [the longest x1 2.78 us: requantized(): (payload * scales[:, :, None]).astype(jnp.bfloat16).reshape(rows, width)]
    gather x3 -> x0, local copies, waits for them, and re-layouts: 21.2 us -> none  [the longest x1 12.1 us: on_device(): expert_out[slot_index].astype(jnp.float32).reshape(tok_rows, TOP, row_width)]
    all_to_all x3 -> x0, starting transfers between devices: 19 us -> none  [the longest x1 7.31 us: on_device(): lax.all_to_all(doubled_scales, 'ep', split_axis=0, concat_axis=0, tiled=T...]
    reduce_sum x2 -> x0, other arithmetic: 12.4 us -> none  [the longest x1 12.4 us: on_device(): return jnp.sum(weights[:, :, None] * per_slot, axis=1).astype(jnp.bfloat16)]
    broadcast_in_dim x3 -> x1, local copies, waits for them, and re-layouts: 10.9 us -> 0.01 us  [on_device(): jnp.where(expert_ids[:, k][None, :] == names, weights[:, k][None, :], 0.0)]
  transfers between devices with their start and end apart: 3 -> 0, of which waited for: 2 -> 0; matrix products, arithmetic and copies ran while one was open for 4% -> 0% of each run, Pallas kernels for 0% -> 0%
where the time goes in v1:
time: 442 us; the launch traced here: 441 us
  Pallas kernels  378 us (86%)
  matrix products  37.5 us (8%)
  local copies, waits for them, and re-layouts  14.7 us (3%)
  other arithmetic  10.5 us (2%)
    pallas_call x1, Pallas kernels, all_tokens(): pl.pallas_call(functools.partial(spread, n), out_shape=(jax.ShapeDtypeStr...  191 us
    pallas_call x1, Pallas kernels, summed(): pl.pallas_call(gather_sums, out_shape=jax.ShapeDtypeStruct((rows, width),...  187 us
    dot_general x1, matrix products, on_device(): partial = jnp.dot(hidden, w_down[0], preferred_element_type=jnp.float32)  14.1 us
    dot_general x1, matrix products, on_device(): upward = jnp.dot(every, w_up[0], preferred_element_type=jnp.float32)  13.3 us
    dot_general x1, matrix products, on_device(): gate = jnp.dot(every, w_gate[0], preferred_element_type=jnp.float32)  10.1 us

profile of v1, /device:TPU:0, one launch (start us, length us, event | category | flops | bytes accessed | tf_op | source)
XLA Modules:
  0.0 441.4 jit_solution(15857207253289437098)
XLA Ops:
  0.0 0.7 reduce_sum.9
  0.7 0.7 broadcast_divide_fusion
  1.4 0.8 slice_bitcast_fusion.3
  2.2 3.7 convert_abs_fusion
  5.8 5.3 %copy.7 = f32[128,7168]{0,1:T(8,128)} copy(f32[128,7168]{1,0:T(8,128)} %convert_abs_fusion) | data formatting | bytes 7340032 | tf_op jit(solution)/shard_map/abs | solution.py:19
  11.1 2.7 reduce_max.9
  13.8 2.0 div.39
  15.9 0.0 copy-start
  15.9 5.4 %copy.8 = f32[128,7168]{1,0:T(8,128)} copy(f32[128,7168]{0,1:T(8,128)} %bitcast.28) | data formatting | bytes 7340032 | tf_op jit(solution)/shard_map/div | solution.py:21
  21.2 0.0 copy-done
  21.2 2.8 multiply_convert_fusion.1.x_ref
  24.0 191.5 %spread.1 = (bf16[8,128,7168]{2,1,0:T(8,128)(2,1)}, f32[8,8,128]{2,1,0:T(8,128)S(1)}) custom-call(bf16[128,7168]{1,0:T(8,128)(2,1)S(1)} %multiply_convert_fusion.1.x_ref, f32[8,128]{1,0:T(8,128)S(1)} %select_add_fusion.share_ref), custom_call_target="tpu_custom_call" | custom-call | tf_op jit(solution)/shard_map/spread/pallas_call | solution.py:131
  215.5 0.0 copy-start.1
  215.5 13.3 %fusion.1 = f32[1024,512]{1,0:T(8,128)S(1)} fusion(bf16[1024,7168]{1,0:T(8,128)(2,1)} %bitcast.31, bf16[1,7168,512]{2,1,0:T(8,128)(2,1)} %param.10), kind=kOutput, calls=%fused_computation.2 | convolution fusion | flops 7516192768 | bytes 24117248 | tf_op jit(solution)/shard_map/dot_general | solution.py:314
  228.8 0.0 copy-done.1
  228.8 10.1 %multiply_convert_fusion.2 = bf16[1024,512]{1,0:T(8,128)(2,1)S(1)} fusion(f32[1024,512]{1,0:T(8,128)S(1)} %fusion.1, bf16[1024,7168]{1,0:T(8,128)(2,1)S(1)} %bitcast.32, bf16[1,7168,512]{2,1,0:T(8,128)(2,1)} %param.9), kind=kOutput, calls=%fused_computation.11 | convolution fusion | flops 7519338496 | bytes 25165824 | tf_op jit(solution)/shard_map/dot_general | solution.py:313
  239.0 14.1 %multiply_convert_fusion = bf16[1024,7168]{1,0:T(8,128)(2,1)} fusion(bf16[1024,512]{1,0:T(8,128)(2,1)S(1)} %multiply_convert_fusion.2, f32[1024]{0:T(1024)S(1)} %bitcast.30, bf16[1,512,7168]{2,1,0:T(8,128)(2,1)} %param.11), kind=kOutput, calls=%fused_computation | convolution fusion | flops 7530872832 | bytes 23072768 | tf_op jit(solution)/shard_map/dot_general | solution.py:316
  253.1 187.0 %gather_sums.1 = bf16[128,7168]{1,0:T(8,128)(2,1)S(1)} custom-call(bf16[8,128,7168]{2,1,0:T(8,128)(2,1)} %bitcast.29), custom_call_target="tpu_custom_call" | custom-call | tf_op jit(solution)/shard_map/gather_sums/pallas_call | solution.py:266
  440.1 1.2 copy.11
  (4 shorter events, 0.1 us)
Async XLA Ops:
  15.9 5.4 %copy-start = (bf16[128,7168]{1,0:T(8,128)(2,1)S(1)}, bf16[128,7168]{1,0:T(8,128)(2,1)}, u32[]{:S(2)}) copy-start(bf16[128,7168]{1,0:T(8,128)(2,1)} %param.6) | copy-start | bytes 5505028
  215.5 13.3 %copy-start.1 = (bf16[8,128,7168]{2,1,0:T(8,128)(2,1)S(1)}, bf16[8,128,7168]{2,1,0:T(8,128)(2,1)}, u32[]{:S(2)}) copy-start(bf16[8,128,7168]{2,1,0:T(8,128)(2,1)} %get-tuple-element.7) | copy-start | bytes 44040196

commit v2 on v1

v2 whole, which is shorter than its diff:
```python
import functools

import jax
import jax.numpy as jnp
from jax import lax
from jax.experimental import pallas as pl
from jax.experimental.pallas import tpu as pltpu
from jax.sharding import PartitionSpec as P

LINE = 4
LANES = 128
MESH = pl.DeviceIdType.MESH
VMEM_LIMIT = 48 * 1024 * 1024


def requantized(tokens):
    rows, width = tokens.shape
    blocks = tokens.astype(jnp.float32).reshape(rows, -1, 16)
    largest = jnp.max(jnp.abs(blocks), axis=2)
    scales = (jnp.maximum(largest, 0.25) / 9.0).astype(jnp.bfloat16).astype(jnp.float32)
    divided = blocks / scales[:, :, None]
    payload = jnp.clip(divided, -6.0, 6.0).astype(jnp.bfloat16).astype(jnp.float32)
    return (payload * scales[:, :, None]).astype(jnp.bfloat16).reshape(rows, width)


def split_of(width):
    return width // LANES // 6 * LANES


def halves_of(rows):
    return pl.ds(0, rows // 2), pl.ds(rows // 2, rows // 2)


def meet(targets):
    barrier = pltpu.get_barrier_semaphore()
    for target in targets:
        pl.semaphore_signal(barrier, inc=1, device_id={"ep": target}, device_id_type=MESH)
    pl.semaphore_wait(barrier, len(targets))


def swap(values, lane, distance):
    high = (lane // distance) % 2 == 1
    width = values.shape[1]
    return jnp.where(
        high, pltpu.roll(values, distance, 1), pltpu.roll(values, width - distance, 1)
    )


def quantize_into(tokens_ref, x_ref):
    rows, width = x_ref.shape

    def body(i, carry):
        at = pl.ds(pl.multiple_of(i * LANES, LANES), LANES)
        values = tokens_ref[:, at].astype(jnp.float32)
        lane = lax.broadcasted_iota(jnp.int32, values.shape, 1)
        largest = jnp.abs(values)
        for distance in (1, 2, 4, 8):
            largest = jnp.maximum(largest, swap(largest, lane, distance))
        scales = (jnp.maximum(largest, 0.25) / 9.0).astype(jnp.bfloat16).astype(jnp.float32)
        payload = jnp.clip(values / scales, -6.0, 6.0).astype(jnp.bfloat16).astype(jnp.float32)
        x_ref[:, at] = (payload * scales).astype(x_ref.dtype)
        return carry

    lax.fori_loop(0, width // LANES, body, 0)


class Copies:
    def __init__(self, send, recv):
        self.send, self.recv, self.numbers = send, recv, {}

    def number(self, name):
        return self.numbers.setdefault(name, len(self.numbers))

    def make(self, name, source, place, target):
        k = self.number(name)
        return pltpu.make_async_remote_copy(
            src_ref=source,
            dst_ref=place,
            send_sem=self.send.at[k],
            recv_sem=self.recv.at[k],
            device_id={"ep": target},
            device_id_type=MESH,
        )


def spread(n, tokens_ref, share_ref, all_ref, shares_ref, x_ref, send, recv, local):
    me = lax.axis_index("ep")
    here, y = me // 2, lax.rem(me, 2)
    other = 1 - y
    peer = 2 * here + other
    rows, width = x_ref.shape
    cut = split_of(width)
    first, second = pl.ds(0, cut), pl.ds(cut, width - cut)
    full, halves = pl.ds(0, rows), halves_of(rows)
    quantize_into(tokens_ref, x_ref)
    keep = pltpu.make_async_copy(x_ref, all_ref.at[me], local.at[0])
    keep_share = pltpu.make_async_copy(share_ref, shares_ref.at[me], local.at[1])
    keep.start()
    keep_share.start()
    meet([lax.rem(me + step, n) for step in range(1, n)])
    all_copies = Copies(send, recv)
    shares = [
        all_copies.make(("share", step), share_ref, shares_ref.at[me], lax.rem(me + step, n))
        for step in range(1, n)
    ]
    last = LINE - 1

    def program(z):
        started = []

        def block(owner, side, rows_of, columns):
            return all_ref.at[2 * owner + side, rows_of, columns]

        def start(name, owner, side, rows_of, columns, target, own=False):
            place = block(owner, side, rows_of, columns)
            source = x_ref.at[rows_of, columns] if own else place
            copy = all_copies.make(name, source, place, target)
            copy.start()
            started.append(copy)

        def wait(name, owner, side, rows_of, columns):
            place = block(owner, side, rows_of, columns)
            all_copies.make(name, place, place, peer).wait_recv()

        def onward(kind, owner, side, rows_of, columns, source_z, own=False):
            for way, ok, step in (("up", z < last, 1), ("down", z > 0, -1)):
                if ok and (source_z - z) * step <= 0:
                    start((kind, way, owner), owner, side, rows_of, columns, 2 * (z + step) + y, own)

        def way_of(owner):
            return "up" if owner < z else "down"

        def pass_b(owner, i):
            own = owner == z
            if not own:
                wait((("b", i), way_of(owner), owner), owner, y, halves[i], second)
            onward(("b", i), owner, y, halves[i], second, owner, own)
            start((("b", i), "peer", owner), owner, y, halves[i], second, peer, own)

        def pass_a(kind, owner, side):
            wait((kind, way_of(owner), owner), owner, side, full, first)
            onward(kind, owner, side, full, first, owner)

        start(("a", "peer"), z, y, full, first, peer, True)
        pass_b(z, 0)
        for copy in shares:
            copy.start()
        pass_b(z, 1)
        onward("a", z, y, full, first, z, True)
        by_distance = [
            [owner for owner in (z - hop, z + hop) if 0 <= owner <= last] for hop in range(1, LINE)
        ]
        for hop in range(LINE - 1):
            for i in range(2):
                for owner in by_distance[hop]:
                    pass_b(owner, i)
            if hop == 1:
                wait(("a", "peer"), z, other, full, first)
                onward("p", z, other, full, first, z)
        for owners in by_distance:
            for owner in owners:
                pass_a("a", owner, y)
            for owner in owners:
                pass_a("p", owner, other)
        for owner in range(LINE):
            for i in range(2):
                wait((("b", i), "peer", owner), owner, other, halves[i], second)
        for copy in started:
            copy.wait_send()

    for z in range(LINE):
        pl.when(here == z)(functools.partial(program, z))
    for copy in shares:
        copy.wait()
    keep.wait()
    keep_share.wait()


def all_tokens(tokens, share):
    n = lax.axis_size("ep")
    rows, width = tokens.shape
    count = 64
    return pl.pallas_call(
        functools.partial(spread, n),
        out_shape=(
            jax.ShapeDtypeStruct((n, rows, width), tokens.dtype),
            jax.ShapeDtypeStruct((n,) + share.shape, share.dtype),
        ),
        in_specs=[pl.BlockSpec(memory_space=pltpu.VMEM)] * 2,
        out_specs=[pl.BlockSpec(memory_space=pl.ANY)] * 2,
        scratch_shapes=[
            pltpu.VMEM((rows, width), tokens.dtype),
            pltpu.SemaphoreType.DMA((count,)),
            pltpu.SemaphoreType.DMA((count,)),
            pltpu.SemaphoreType.DMA((2,)),
        ],
        compiler_params=pltpu.CompilerParams(
            collective_id=0, has_side_effects=True, vmem_limit_bytes=VMEM_LIMIT
        ),
        name="spread",
    )(tokens, share)


def add_up(target, sources):
    rows = target.shape[0]
    step = 16

    def body(i, carry):
        at = pl.ds(pl.multiple_of(i * step, step), step)
        total = sources[0][at, :].astype(jnp.float32)
        for source in sources[1:]:
            total = total + source[at, :].astype(jnp.float32)
        target[at, :] = total.astype(target.dtype)
        return carry

    lax.fori_loop(0, rows // step, body, 0)


def gather_sums(
    c_ref, out_ref, own_b, own_a, got_b, zed_b, zed_a, got_a3, send, recv, local
):
    me = lax.axis_index("ep")
    here, y = me // 2, lax.rem(me, 2)
    other = 1 - y
    peer = 2 * here + other
    rows, width = out_ref.shape
    cut = split_of(width)
    first, second = pl.ds(0, cut), pl.ds(cut, width - cut)
    halves = halves_of(rows)
    faces = (other, y)
    last = LINE - 1
    loads = []

    def load(owner, columns, place):
        k = len(loads)
        loads.append(pltpu.make_async_copy(c_ref.at[owner, :, columns], place, local.at[k]))
        loads[k].start()

    for d in range(LINE):
        for i in range(2):
            load(2 * d + faces[i], first, own_a.at[d, i])
    for d in range(LINE):
        load(2 * d + y, second, own_b.at[d])
    meet([lax.rem(me + step, 2 * LINE) for step in range(1, 2 * LINE)])
    all_copies = Copies(send, recv)

    def program(z):
        started = []
        if z in (0, last):
            order = sorted((d for d in range(LINE) if d != z), key=lambda d: -abs(d - z))
        else:
            far, near = (last, 0) if z < last - z else (0, last)
            order = [far, near] + [d for d in range(1, last) if d != z]

        def send_off(name, source, place, target):
            copy = all_copies.make(name, source, place, target)
            copy.start()
            started.append(copy)

        def wait(name, place):
            all_copies.make(name, place, place, peer).wait_recv()

        def feeders(d):
            found = []
            if z > 0 and d >= z:
                found.append(0)
            if z < last and d <= z:
                found.append(1)
            return found

        def take_a(d, i):
            found = feeders(d)
            for way in found:
                wait(("a", way, d, i), zed_a.at[way, d, i])
            return [zed_a.at[way, d, i] for way in found]

        def take_b(d, h):
            wait(("y", d, h), got_b.at[d, halves[h]])
            found = feeders(d)
            for way in found:
                wait(("b", way, d, h), zed_b.at[way, d, halves[h]])
            return [got_b.at[d, halves[h]]] + [zed_b.at[way, d, halves[h]] for way in found]

        def pass_a(d):
            way, target = (0, 2 * (z + 1) + y) if d > z else (1, 2 * (z - 1) + y)
            for i in range(2):
                sources = take_a(d, i)
                if sources:
                    add_up(own_a.at[d, i], [own_a.at[d, i]] + sources)
                send_off(("a", way, d, i), own_a.at[d, i], zed_a.at[way, d, i], target)

        def pass_b(d):
            way, target = (0, 2 * (z + 1) + y) if d > z else (1, 2 * (z - 1) + y)
            for h in range(2):
                mine = own_b.at[d, halves[h]]
                add_up(mine, [mine] + take_b(d, h))
                send_off(("b", way, d, h), mine, zed_b.at[way, d, halves[h]], target)

        for d in order + [z]:
            for h in range(2):
                send_off(
                    ("y", d, h),
                    c_ref.at[2 * d + other, halves[h], second],
                    got_b.at[d, halves[h]],
                    peer,
                )
        for copy in loads:
            copy.wait()
        for d in order:
            pass_a(d)
        rest = order
        if z in (0, last):
            pass_b(order[0])
            rest = order[1:]
        add_up(own_a.at[z, 0], [own_a.at[z, 0]] + take_a(z, 0))
        send_off("a3", own_a.at[z, 0], got_a3, peer)
        ends = take_a(z, 1)
        for d in rest:
            pass_b(d)
        for h in range(2):
            add_up(out_ref.at[halves[h], second], [own_b.at[z, halves[h]]] + take_b(z, h))
        wait("a3", got_a3)
        add_up(out_ref.at[:, first], [own_a.at[z, 1], got_a3] + ends)
        for copy in started:
            copy.wait_send()

    for z in range(LINE):
        pl.when(here == z)(functools.partial(program, z))


def summed(scaled):
    n, rows, width = scaled.shape
    cut = split_of(width)
    rest = width - cut
    kind = scaled.dtype
    count = 48
    return pl.pallas_call(
        gather_sums,
        out_shape=jax.ShapeDtypeStruct((rows, width), kind),
        in_specs=[pl.BlockSpec(memory_space=pl.ANY)],
        out_specs=pl.BlockSpec(memory_space=pltpu.VMEM),
        scratch_shapes=[
            pltpu.VMEM((LINE, rows, rest), kind),
            pltpu.VMEM((LINE, 2, rows, cut), kind),
            pltpu.VMEM((LINE, rows, rest), kind),
            pltpu.VMEM((2, LINE, rows, rest), kind),
            pltpu.VMEM((2, LINE, 2, rows, cut), kind),
            pltpu.VMEM((rows, cut), kind),
            pltpu.SemaphoreType.DMA((count,)),
            pltpu.SemaphoreType.DMA((count,)),
            pltpu.SemaphoreType.DMA((3 * LINE,)),
        ],
        compiler_params=pltpu.CompilerParams(
            collective_id=1, has_side_effects=True, vmem_limit_bytes=VMEM_LIMIT
        ),
        name="gather_sums",
    )(scaled)


def on_device(tokens, expert_ids, affinity, w_gate, w_up, w_down):
    n = lax.axis_size("ep")
    experts = n // 2
    own = lax.axis_index("ep") // 2
    rows, width = tokens.shape
    weights = affinity / jnp.sum(affinity, axis=1, keepdims=True)
    padded = -(-experts // 8) * 8
    names = jnp.arange(padded, dtype=jnp.int32)[:, None]
    shares = sum(
        jnp.where(expert_ids[:, k][None, :] == names, weights[:, k][None, :], 0.0)
        for k in range(weights.shape[1])
    )
    by_line = experts == LINE and rows % 32 == 0 and width % LANES == 0
    if by_line:
        every, shares = all_tokens(tokens, shares)
    else:
        every = lax.all_gather(requantized(tokens), "ep", axis=0, tiled=False)
        shares = lax.all_gather(shares, "ep", axis=0, tiled=False)
    every = every.reshape(n * rows, width)
    share = lax.dynamic_slice_in_dim(shares, own, 1, axis=1).reshape(n * rows, 1)
    gate = jnp.dot(every, w_gate[0], preferred_element_type=jnp.float32)
    upward = jnp.dot(every, w_up[0], preferred_element_type=jnp.float32)
    hidden = (jax.nn.silu(gate) * upward).astype(jnp.bfloat16)
    partial = jnp.dot(hidden, w_down[0], preferred_element_type=jnp.float32)
    scaled = (partial * share).astype(jnp.bfloat16)
    if by_line:
        return summed(scaled.reshape(n, rows, width))
    return lax.psum_scatter(scaled, "ep", scatter_dimension=0, tiled=True)


def solution(mesh):
    in_specs = (
        P(("dp", "ep"), None),
        P(("dp", "ep"), None),
        P(("dp", "ep"), None),
        P("ep", None, None),
        P("ep", None, None),
        P("ep", None, None),
    )
    return jax.shard_map(
        on_device, mesh=mesh, in_specs=in_specs, out_specs=P(("dp", "ep"), None), check_vma=False
    )
```

time: 442 us -> 350 us (0.79)
  Pallas kernels: 378 us -> 309 us
  local copies, waits for them, and re-layouts: 14.7 us -> 3.79 us
  other arithmetic: 10.5 us -> 1.38 us
    pallas_call x1, Pallas kernels: 187 us -> 141 us  [summed(): pl.pallas_call(gather_sums, out_shape=jax.ShapeDtypeStruct((rows, width),...]
    pallas_call x1, Pallas kernels: 191 us -> 167 us  [all_tokens(): pl.pallas_call(functools.partial(spread, n), out_shape=(jax.ShapeDtypeStr...]
    div x2 -> x0, local copies, waits for them, and re-layouts: 7.41 us -> none  [requantized(): divided = blocks / scales[:, :, None]]
    abs x1 -> x0, local copies, waits for them, and re-layouts: 5.28 us -> none  [requantized(): largest = jnp.max(jnp.abs(blocks), axis=2)]
where the time goes in v2:
time: 350 us; the launch traced here: 349 us
  Pallas kernels  309 us (88%)
  matrix products  35.5 us (10%)
  local copies, waits for them, and re-layouts  3.79 us (1%)
    pallas_call x1, Pallas kernels, all_tokens(): pl.pallas_call(functools.partial(spread, n), out_shape=(jax.ShapeDtypeStr...  167 us
    pallas_call x1, Pallas kernels, summed(): pl.pallas_call(gather_sums, out_shape=jax.ShapeDtypeStruct((rows, width),...  141 us
    dot_general x1, matrix products, on_device(): partial = jnp.dot(hidden, w_down[0], preferred_element_type=jnp.float32)  14.1 us
    dot_general x1, matrix products, on_device(): upward = jnp.dot(every, w_up[0], preferred_element_type=jnp.float32)  13.4 us
    dot_general x1, matrix products, on_device(): gate = jnp.dot(every, w_gate[0], preferred_element_type=jnp.float32)  8.02 us

profile of v2, /device:TPU:0, one launch (start us, length us, event | category | flops | bytes accessed | tf_op | source)
XLA Modules:
  0.0 349.3 jit_solution(353805059606021604)
XLA Ops:
  0.0 0.7 reduce_sum.9
  0.7 0.7 broadcast_divide_fusion
  1.4 0.8 slice_bitcast_fusion.3
  2.2 0.0 copy-start
  2.2 1.5 copy-done
  3.7 167.3 %spread.1 = (bf16[8,128,7168]{2,1,0:T(8,128)(2,1)}, f32[8,8,128]{2,1,0:T(8,128)S(1)}) custom-call(bf16[128,7168]{1,0:T(8,128)(2,1)S(1)} %copy-done, f32[8,128]{1,0:T(8,128)S(1)} %select_add_fusion.share_ref), custom_call_target="tpu_custom_call" | custom-call | tf_op jit(solution)/shard_map/spread/pallas_call | solution.py:183
  171.0 0.0 copy-start.1
  171.0 0.0 copy-start.2
  171.0 13.4 %fusion.1 = f32[1024,512]{1,0:T(8,128)S(1)} fusion(bf16[1024,7168]{1,0:T(8,128)(2,1)} %bitcast.27, bf16[1,7168,512]{2,1,0:T(8,128)(2,1)} %param.10), kind=kOutput, calls=%fused_computation.2 | convolution fusion | flops 7516192768 | bytes 24117248 | tf_op jit(solution)/shard_map/dot_general | solution.py:381
  184.4 0.0 copy-done.1
  184.4 0.3 copy-done.2
  184.6 8.0 %multiply_convert_fusion.1 = bf16[1024,512]{1,0:T(8,128)(2,1)S(1)} fusion(f32[1024,512]{1,0:T(8,128)S(1)} %fusion.1, bf16[1024,7168]{1,0:T(8,128)(2,1)S(1)} %bitcast.28, bf16[1,7168,512]{2,1,0:T(8,128)(2,1)S(1)} %copy-done.2), kind=kOutput, calls=%fused_computation.6 | convolution fusion | flops 7519338496 | bytes 25165824 | tf_op jit(solution)/shard_map/dot_general | solution.py:380
  192.7 14.1 %multiply_convert_fusion = bf16[1024,7168]{1,0:T(8,128)(2,1)} fusion(bf16[1024,512]{1,0:T(8,128)(2,1)S(1)} %multiply_convert_fusion.1, f32[1024]{0:T(1024)S(1)} %bitcast.26, bf16[1,512,7168]{2,1,0:T(8,128)(2,1)} %param.11), kind=kOutput, calls=%fused_computation | convolution fusion | flops 7530872832 | bytes 23072768 | tf_op jit(solution)/shard_map/dot_general | solution.py:383
  206.8 141.3 %gather_sums.1 = bf16[128,7168]{1,0:T(8,128)(2,1)S(1)} custom-call(bf16[8,128,7168]{2,1,0:T(8,128)(2,1)} %bitcast.25), custom_call_target="tpu_custom_call" | custom-call | tf_op jit(solution)/shard_map/gather_sums/pallas_call | solution.py:337
  348.1 1.2 copy.8
  (3 shorter events, 0.0 us)
Async XLA Ops:
  2.2 1.5 copy-start
  171.0 13.4 %copy-start.1 = (bf16[8,128,7168]{2,1,0:T(8,128)(2,1)S(1)}, bf16[8,128,7168]{2,1,0:T(8,128)(2,1)}, u32[]{:S(2)}) copy-start(bf16[8,128,7168]{2,1,0:T(8,128)(2,1)} %get-tuple-element.7) | copy-start | bytes 44040196
  171.0 13.7 %copy-start.2 = (bf16[1,7168,512]{2,1,0:T(8,128)(2,1)S(1)}, bf16[1,7168,512]{2,1,0:T(8,128)(2,1)}, u32[]{:S(2)}) copy-start(bf16[1,7168,512]{2,1,0:T(8,128)(2,1)} %param.9) | copy-start | bytes 22020100
